TPU v7x, 32 devices: a whole 2x2x4 slice. The times are simulated.
32 devices in a mesh: grp: 2 (over x), az: 8 (over z, y), ax: 2 (over core).
Axes of the slice: x: 2, y: 2, z: 4, core: 2. Of those that a mesh axis runs over, the one named last changes fastest.
Arguments:
- cavity_block: float32 [8, 96, 32, 256], P(None, 'grp', 'az', 'ax'), may hold values from -95 to 95
- shell_block: float32 [8, 6, 32, 256], P(None, None, 'az', 'ax'), may hold values from -95 to 95
- column_matrix: float32 [2, 48, 48], P('grp'), may hold values from -2 to 6, as said below
- shell_matrix: float32 [6, 6], replicated, may hold values from -2 to 6, as said below
- shifted_diagonal: float32 [96, 32, 256], P('grp', 'az', 'ax'), may hold values from 1.6 to 3
- shell_diagonal: float32 [6, 32, 256], P(None, 'az', 'ax'), may hold values from 1.6 to 3
- wet_area: float32 [32, 256], P('az', 'ax'), may hold values from 0.3 to 1.5
Outputs:
- cavity_solution: float32 [8, 96, 32, 256], P(None, 'grp', 'az', 'ax')
- cavity_residual: float32 [8, 96, 32, 256], P(None, 'grp', 'az', 'ax')
- shell_solution: float32 [8, 6, 32, 256], P(None, None, 'az', 'ax')
- shell_residual: float32 [8, 6, 32, 256], P(None, None, 'az', 'ax')
Inputs may be any that keep to these rules, and one draw needn't show every extreme that they name: `column_matrix`: each symmetric and positive definite. `shell_matrix`: symmetric and positive definite.
All inputs are finite; a program needn't handle non-finite values.
Results may differ from a plain program's by a relative error of at most 0.0015.
Values sent between devices are 32-bit elements; how exact they have to be, the bound alone decides.
No kernel may reach another device: no remote copies, remote signals or barrier semaphores. Data moves between devices by JAX's collectives and lax.ppermute only.
A program may use at most 128 MiB of HBM per device.

v0:
```python
import jax
import jax.numpy as jnp
from jax import lax
from jax.sharding import PartitionSpec as P

ITERS = 3
exact_mode = lax.Precision.HIGHEST


def swapped(block, axis, apart):
    count = lax.axis_size(axis)
    route = []
    for low in range(count):
        high = low | 1 << apart
        if high != low and high < count:
            route += [(low, high), (high, low)]
    return lax.ppermute(block, axis, route)


def extended(array, sides, width, wrap):
    for axis, dim in sides:
        peers, length = (lax.axis_size(axis), array.shape[dim])
        up = [(i, (i + 1) % peers) for i in range(peers if wrap else peers - 1)]
        down = [(j, i) for i, j in up]
        last = lax.slice_in_dim(array, length - width, length, axis=dim)
        first = lax.slice_in_dim(array, 0, width, axis=dim)
        before = lax.ppermute(last, axis, up)
        after = lax.ppermute(first, axis, down)
        array = jnp.concatenate([before, array, after], axis=dim)
    return array


def solve_posdef(gram_matrix, targets):
    factor = jnp.linalg.cholesky(gram_matrix)
    middle = lax.linalg.triangular_solve(factor, targets, left_side=True, lower=True)
    return lax.linalg.triangular_solve(factor, middle, left_side=True, lower=True, transpose_a=True)


def products(first_set, second_set):
    return jnp.einsum("vrax,wrax->vw", first_set, second_set, precision=exact_mode)


def combine(vector_set, mixing):
    return jnp.einsum("vrax,vw->wrax", vector_set, mixing, precision=exact_mode)


def column_part(vector_set, matrix):
    flat_set = vector_set.reshape(vector_set.shape[0], vector_set.shape[1], -1)
    mixed_set = jnp.einsum("rs,vsc->vrc", matrix, flat_set, precision=exact_mode)
    return mixed_set.reshape(vector_set.shape)


def coupled(result, vector_set, wet_area, layout):
    half, interface_row, outer_flag = layout
    iface_own = lax.dynamic_slice_in_dim(vector_set, interface_row, 1, 1)
    wall_own = vector_set[:, half - 1 : half]
    sent = jnp.concatenate([iface_own, wall_own], axis=1)
    received = swapped(sent, "grp", 0)
    result_row = lax.dynamic_slice_in_dim(result, interface_row, 1, 1)
    result = lax.dynamic_update_slice_in_dim(
        result, result_row - received[:, 0:1], interface_row, 1
    )
    wall = outer_flag * wall_own + (1.0 - outer_flag) * received[:, 1:2]
    shell_top = vector_set[:, half : half + 1]
    result = result.at[:, half - 1 : half].add(-outer_flag * wet_area * shell_top)
    result = result.at[:, half : half + 1].add(-wet_area * wall)
    return result


def apply_shallow(vector_set, matrix, diagonal_set, wet_area, layout):
    beside_all = extended(vector_set, (("az", 2),), 1, True)
    along = extended(vector_set, (("ax", 3),), 1, False)
    neighbours = beside_all[:, :, 2:] + beside_all[:, :, :-2] + along[..., 2:] + along[..., :-2]
    result = column_part(vector_set, matrix) + (4.0 + diagonal_set) * vector_set - neighbours
    return coupled(result, vector_set, wet_area, layout)


def per_device(
    cavity_block,
    shell_block,
    column_matrix,
    shell_matrix,
    shifted_diagonal,
    shell_diagonal,
    wet_area,
):
    group_index = lax.axis_index("grp")
    outer_flag = (group_index == 1).astype(jnp.float32)
    shell_share = 1.0 - outer_flag
    half = column_matrix.shape[1]
    shell_rows = shell_matrix.shape[0]
    interface_row = jnp.where(group_index == 1, 0, half - 1).astype(jnp.int32)
    layout = (half, interface_row, outer_flag)
    upper = jnp.concatenate([column_matrix[0], jnp.zeros((half, shell_rows), jnp.float32)], axis=1)
    lower = jnp.concatenate([jnp.zeros((shell_rows, half), jnp.float32), shell_matrix], axis=1)
    matrix = jnp.concatenate([upper, lower], axis=0)
    right_side = jnp.concatenate([cavity_block, shell_block], axis=1)
    diagonal_own = jnp.concatenate([shifted_diagonal, shell_diagonal], axis=0)

    def moments_local(first_set, second_set):
        cavity_part = products(first_set[:, :half], second_set[:, :half])
        return cavity_part + shell_share * products(first_set[:, half:], second_set[:, half:])

    residual = right_side
    direction = right_side
    solution = jnp.zeros_like(right_side)
    start_core = residual
    norms_now = lax.psum(moments_local(start_core, start_core), ("grp", "az", "ax"))
    for sweep in range(ITERS):
        image_set = apply_shallow(direction, matrix, diagonal_own, wet_area, layout)
        direction_core = direction
        residual_core = residual
        curvature, crossing, squares = lax.psum(
            (
                moments_local(direction_core, image_set),
                moments_local(image_set, residual_core),
                moments_local(image_set, image_set),
            ),
            ("grp", "az", "ax"),
        )
        step_mix = solve_posdef(curvature, norms_now)
        norms_next = norms_now - jnp.dot(step_mix.T, crossing, precision=exact_mode)
        norms_next = norms_next - jnp.dot(crossing.T, step_mix, precision=exact_mode)
        norms_next = norms_next + jnp.dot(
            jnp.dot(step_mix.T, squares, precision=exact_mode), step_mix, precision=exact_mode
        )
        solution = solution + combine(direction_core, step_mix)
        residual = residual - combine(image_set, step_mix)
        if sweep + 1 < ITERS:
            turn_mix = solve_posdef(norms_now, norms_next)
            direction = residual + combine(direction, turn_mix)
            norms_now = norms_next
    return (solution[:, :half], residual[:, :half], solution[:, half:], residual[:, half:])


def solution(mesh):
    return jax.shard_map(
        per_device,
        mesh=mesh,
        in_specs=(
            P(None, "grp", "az", "ax"),
            P(None, None, "az", "ax"),
            P("grp", None, None),
            P(),
            P("grp", "az", "ax"),
            P(None, "az", "ax"),
            P("az", "ax"),
        ),
        out_specs=(
            P(None, "grp", "az", "ax"),
            P(None, "grp", "az", "ax"),
            P(None, None, "az", "ax"),
            P(None, None, "az", "ax"),
        ),
        check_vma=False,
    )
```

profile of v0, /device:TPU:0, one launch (start us, length us, event | category | flops | bytes accessed | tf_op | source)
XLA Modules:
  0.0 250.7 jit_solution(17498085943303923312)
XLA Ops:
  0.6 2.5 fusion.124
  4.1 1.0 copy.166
  5.1 2.4 collective-permute-start.3
  7.9 1.3 collective-permute-start.2
  9.2 0.8 fusion.122
  10.0 2.3 collective-permute-start.1
  12.3 3.0 %collective-permute-start = (f32[8,54,1,128]{3,0,1,2:T(8,128)}, f32[8,54,1,128]{3,0,1,2:T(8,128)}, u32[]{:S(2)}, u32[]{:S(2)}) collective-permute-start(f32[8,54,1,128]{3,0,1,2:T(8,128)} %get-tuple-element.110), channel_id=1, source_target_pairs={{2,0},{4,2},{6,4},{8,6},{10,8},{12,10},{14,12},{0,14},{3,1},{5,3},... | collective-permute-start | bytes 663560 | tf_op jit(solution)/shard_map/ppermute | solution.py:28
  16.7 1.7 collective-permute-start.4
  18.4 1.9 convolution_bitcast_fusion.3
  20.4 0.9 fusion.13
  21.4 2.4 convolution_bitcast_fusion.2
  24.9 1.4 copy.165
  26.3 2.5 fusion.26
  30.2 0.7 fusion.61
  31.0 1.9 convolution_bitcast_fusion.15
  32.9 1.8 convolution_bitcast_fusion.13
  35.7 38.6 %all-reduce.3 = (f32[8,8]{0,1:T(8,128)S(1)}, f32[8,8]{1,0:T(8,128)S(1)}, f32[8,8]{0,1:T(8,128)S(1)}, f32[8,8]{0,1:T(8,128)S(1)}) all-reduce(f32[8,8]{0,1:T(8,128)S(1)} %copy-done.18, f32[8,8]{1,0:T(8,128)S(1)} %bitcast.241, f32[8,8]{0,1:T(8,128)S(1)} %fusion.11, ...), channel_id=1, replica_groups=mesh['grp'=2,'az'=8,'ax'=2] {'grp','az','ax'}, use_global_device_ids=true, to_apply=%region_3.0 | all-reduce | flops 256 | bytes 2048 | tf_op jit(solution)/shard_map/psum | solution.py:108
  77.5 1.9 fusion.31
  79.4 0.9 convolution_subtract_fusion.2
  84.2 0.9 convolution_add_fusion.3
  85.0 1.2 fusion.121
  86.3 0.8 fusion.120
  88.4 2.1 copy.206
  90.6 1.9 collective-permute-start.8
  92.4 1.0 copy.204
  93.4 1.3 collective-permute-start.7
  94.7 2.4 collective-permute-start.6
  97.1 2.4 collective-permute-start.5
  99.5 3.1 %convolution_bitcast_fusion.1 = f32[8,54,512]{2,1,0:T(8,128)} fusion(f32[8,54,512]{2,0,1:T(8,128)S(1)} %bitcast.235, f32[6,6]{1,0:T(8,128)S(1)} %copy-done.14, f32[48,48]{1,0:T(8,128)} %bitcast.238), kind=kOutput, calls=%fused_computation.1 | convolution fusion | flops 143341808 | bytes 1778832 | tf_op jit(solution)/shard_map/rs,vsc->vrc/dot_general | solution.py:49
  103.3 2.3 collective-permute-start.9
  107.6 1.2 custom-call.23
  108.9 1.1 copy.207
  110.0 1.3 copy.205
  112.0 2.5 fusion.22
  116.0 1.8 convolution_bitcast_fusion.11
  117.8 1.8 convolution_bitcast_fusion.9
  119.6 1.8 convolution_bitcast_fusion.7
  122.3 37.7 %all-reduce.2 = (f32[8,8]{0,1:T(8,128)S(1)}, f32[8,8]{0,1:T(8,128)}, f32[8,8]{0,1:T(8,128)}) all-reduce(f32[8,8]{0,1:T(8,128)S(1)} %fusion.7, f32[8,8]{0,1:T(8,128)S(1)} %fusion.5, f32[8,8]{0,1:T(8,128)S(1)} %fusion.3), channel_id=1, replica_groups=mesh['grp'=2,'az'=8,'ax'=2] {'grp','az','ax'}, use_global_device_ids=true, to_apply=%region_6.10 | all-reduce | flops 192 | bytes 1536 | tf_op jit(solution)/shard_map/psum | solution.py:113
  163.1 0.9 convolution_subtract_fusion.1
  166.0 0.9 convolution_add_fusion.1
  166.8 1.5 fusion.119
  168.3 0.8 fusion.118
  169.2 1.1 copy-done.2
  170.3 1.9 convolution_add_fusion.2
  172.1 2.2 copy.237
  174.4 2.0 collective-permute-start.13
  176.3 1.0 copy.235
  177.3 1.3 collective-permute-start.12
  178.6 2.7 %collective-permute-start.11 = (f32[8,54,1,128]{3,0,1,2:T(8,128)}, f32[8,54,1,128]{3,0,1,2:T(8,128)S(1)}, u32[]{:S(2)}, u32[]{:S(2)}) collective-permute-start(f32[8,54,1,128]{3,0,1,2:T(8,128)} %get-tuple-element.101), channel_id=1, source_target_pairs={{0,2},{2,4},{4,6},{6,8},{8,10},{10,12},{12,14},{14,0},{1,3},{3,5},... | collective-permute-start | bytes 663560 | tf_op jit(solution)/shard_map/ppermute | solution.py:27
  181.3 2.1 collective-permute-start.10
  183.4 3.1 %convolution_bitcast_fusion = f32[8,54,512]{2,1,0:T(8,128)} fusion(f32[8,54,512]{2,0,1:T(8,128)S(1)} %bitcast.236, f32[6,6]{1,0:T(8,128)S(1)} %copy-done.14, f32[48,48]{1,0:T(8,128)} %bitcast.239), kind=kOutput, calls=%fused_computation | convolution fusion | flops 143341808 | bytes 1778832 | tf_op jit(solution)/shard_map/rs,vsc->vrc/dot_general | solution.py:49
  187.1 2.2 collective-permute-start.14
  189.3 1.1 copy.238
  190.5 1.3 copy.236
  192.7 1.8 collective-permute-done.10
  194.5 2.4 fusion.18
  198.5 1.8 convolution_bitcast_fusion.5
  200.5 38.7 %psum.63 = f32[8,8]{0,1:T(8,128)S(1)} all-reduce(f32[8,8]{0,1:T(8,128)S(1)} %fusion.1), channel_id=1, replica_groups=mesh['grp'=2,'az'=8,'ax'=2] {'grp','az','ax'}, use_global_device_ids=true, to_apply=%region_9.13 | all-reduce | flops 64 | bytes 512 | tf_op jit(solution)/shard_map/psum | solution.py:113
  242.4 0.9 convolution_subtract_fusion
  243.6 0.8 convolution_add_fusion
  244.5 1.0 copy-done.4
  245.4 1.1 slice-done.2
  246.6 1.1 copy.249
  247.8 1.4 copy.250
  (149 shorter events, 34.2 us)
Async XLA Ops:
  0.6 2.5 %copy-start.6 = (f32[8,6,4,128]{3,2,1,0:T(4,128)S(1)}, f32[8,6,4,128]{3,2,1,0:T(4,128)}, u32[]{:S(2)}) copy-start(f32[8,6,4,128]{3,2,1,0:T(4,128)} %param.25) | copy-start | bytes 294916
  5.1 19.4 %collective-permute-start.3 = (f32[8,54,4,1]{1,0,3,2:T(8,128)}, f32[8,54,4,1]{1,0,3,2:T(8,128)S(1)}, u32[]{:S(2)}, u32[]{:S(2)}) collective-permute-start(f32[8,54,4,1]{1,0,3,2:T(8,128)} %copy.166), channel_id=1, source_target_pairs={{0,1},{2,3},{4,5},{6,7},{8,9},{10,11},{12,13},{14,15},{16,17},{18,... | collective-permute-start | bytes 20744 | tf_op jit(solution)/shard_map/ppermute | solution.py:27
  7.5 10.9 %copy-start = (f32[8,48,4,128]{3,2,1,0:T(4,128)S(1)}, f32[8,48,4,128]{3,2,1,0:T(4,128)}, u32[]{:S(2)}) copy-start(f32[8,48,4,128]{3,2,1,0:T(4,128)} %param.24) | copy-start | bytes 2359300
  7.9 17.0 %collective-permute-start.2 = (f32[8,54,4,1]{1,0,3,2:T(8,128)S(1)}, f32[8,54,4,1]{1,0,3,2:T(8,128)S(1)}, u32[]{:S(2)}, u32[]{:S(2)}) collective-permute-start(f32[8,54,4,1]{1,0,3,2:T(8,128)S(1)} %copy.164), channel_id=1, source_target_pairs={{1,0},{3,2},{5,4},{7,6},{9,8},{11,10},{13,12},{15,14},{17,16},{19,... | collective-permute-start | bytes 20744 | tf_op jit(solution)/shard_map/ppermute | solution.py:28
  10.0 16.3 %collective-permute-start.1 = (f32[8,54,1,128]{3,0,1,2:T(8,128)}, f32[8,54,1,128]{3,0,1,2:T(8,128)}, u32[]{:S(2)}, u32[]{:S(2)}) collective-permute-start(f32[8,54,1,128]{3,0,1,2:T(8,128)} %get-tuple-element.111), channel_id=1, source_target_pairs={{0,2},{2,4},{4,6},{6,8},{8,10},{10,12},{12,14},{14,0},{1,3},{3,5},... | collective-permute-start | bytes 663560 | tf_op jit(solution)/shard_map/ppermute | solution.py:27
  12.3 14.0 %collective-permute-start = (f32[8,54,1,128]{3,0,1,2:T(8,128)}, f32[8,54,1,128]{3,0,1,2:T(8,128)}, u32[]{:S(2)}, u32[]{:S(2)}) collective-permute-start(f32[8,54,1,128]{3,0,1,2:T(8,128)} %get-tuple-element.110), channel_id=1, source_target_pairs={{2,0},{4,2},{6,4},{8,6},{10,8},{12,10},{14,12},{0,14},{3,1},{5,3},... | collective-permute-start | bytes 663560 | tf_op jit(solution)/shard_map/ppermute | solution.py:28
  16.7 12.1 %collective-permute-start.4 = (f32[8,2,4,128]{3,0,1,2:T(8,128)}, f32[8,2,4,128]{3,0,1,2:T(8,128)}, u32[]{:S(2)}, u32[]{:S(2)}) collective-permute-start(f32[8,2,4,128]{3,0,1,2:T(8,128)} %pad_maximum_fusion.12), channel_id=1, source_target_pairs={{0,16},{16,0},{1,17},{17,1},{2,18},{18,2},{3,19},{19,3},{4,20},{20... | collective-permute-start | bytes 98312 | tf_op jit(solution)/shard_map/ppermute | solution.py:17
  20.4 0.9 copy-start.8
  20.4 0.9 copy-start.14
  21.3 2.4 copy-start.21
  21.3 2.4 copy-start.11
  21.4 2.4 copy-start.19
  32.9 1.8 copy-start.7
  34.9 0.7 copy-start.18
  90.6 18.3 %collective-permute-start.8 = (f32[8,54,4,1]{1,0,3,2:T(8,128)}, f32[8,54,4,1]{1,0,3,2:T(8,128)}, u32[]{:S(2)}, u32[]{:S(2)}) collective-permute-start(f32[8,54,4,1]{1,0,3,2:T(8,128)} %copy.206), channel_id=1, source_target_pairs={{0,1},{2,3},{4,5},{6,7},{8,9},{10,11},{12,13},{14,15},{16,17},{18,... | collective-permute-start | bytes 20744 | tf_op jit(solution)/shard_map/ppermute | solution.py:27
  93.4 16.6 %collective-permute-start.7 = (f32[8,54,4,1]{1,0,3,2:T(8,128)}, f32[8,54,4,1]{1,0,3,2:T(8,128)S(1)}, u32[]{:S(2)}, u32[]{:S(2)}) collective-permute-start(f32[8,54,4,1]{1,0,3,2:T(8,128)} %copy.204), channel_id=1, source_target_pairs={{1,0},{3,2},{5,4},{7,6},{9,8},{11,10},{13,12},{15,14},{17,16},{19,... | collective-permute-start | bytes 20744 | tf_op jit(solution)/shard_map/ppermute | solution.py:28
  94.7 16.6 %collective-permute-start.6 = (f32[8,54,1,128]{3,0,1,2:T(8,128)}, f32[8,54,1,128]{3,0,1,2:T(8,128)S(1)}, u32[]{:S(2)}, u32[]{:S(2)}) collective-permute-start(f32[8,54,1,128]{3,0,1,2:T(8,128)} %get-tuple-element.107), channel_id=1, source_target_pairs={{0,2},{2,4},{4,6},{6,8},{8,10},{10,12},{12,14},{14,0},{1,3},{3,5},... | collective-permute-start | bytes 663560 | tf_op jit(solution)/shard_map/ppermute | solution.py:27
  97.1 14.9 %collective-permute-start.5 = (f32[8,54,1,128]{3,0,1,2:T(8,128)}, f32[8,54,1,128]{3,0,1,2:T(8,128)}, u32[]{:S(2)}, u32[]{:S(2)}) collective-permute-start(f32[8,54,1,128]{3,0,1,2:T(8,128)} %get-tuple-element.106), channel_id=1, source_target_pairs={{2,0},{4,2},{6,4},{8,6},{10,8},{12,10},{14,12},{0,14},{3,1},{5,3},... | collective-permute-start | bytes 663560 | tf_op jit(solution)/shard_map/ppermute | solution.py:28
  99.5 3.2 %copy-start.12 = (f32[8,1,4,128]{3,0,1,2:T(8,128)S(1)}, f32[8,1,4,128]{3,0,1,2:T(8,128)}, u32[]{:S(2)}) copy-start(f32[8,1,4,128]{3,0,1,2:T(8,128)} %get-tuple-element.104) | copy-start | bytes 49156
  99.5 3.2 %copy-start.13 = (f32[8,1,4,128]{3,0,1,2:T(8,128)S(1)}, f32[8,1,4,128]{3,0,1,2:T(8,128)}, u32[]{:S(2)}) copy-start(f32[8,1,4,128]{3,0,1,2:T(8,128)} %get-tuple-element.105) | copy-start | bytes 49156
  102.7 2.9 %copy-start.16 = (f32[8,8]{1,0:T(8,128)S(1)}, f32[8,8]{1,0:T(8,128)}, u32[]{:S(2)}) copy-start(f32[8,8]{1,0:T(8,128)} %copy.218) | copy-start | bytes 772
  103.3 11.2 %collective-permute-start.9 = (f32[8,2,4,128]{3,0,1,2:T(8,128)}, f32[8,2,4,128]{3,0,1,2:T(8,128)}, u32[]{:S(2)}, u32[]{:S(2)}) collective-permute-start(f32[8,2,4,128]{3,0,1,2:T(8,128)} %pad_maximum_fusion.13), channel_id=1, source_target_pairs={{0,16},{16,0},{1,17},{17,1},{2,18},{18,2},{3,19},{19,3},{4,20},{20... | collective-permute-start | bytes 98312 | tf_op jit(solution)/shard_map/ppermute | solution.py:17
  111.3 0.7 copy-start.9
  163.1 0.9 copy-start.17
  164.0 0.7 copy-start.20
  164.9 0.7 copy-start.15
  169.1 1.2 copy-start.2
  172.1 4.2 %copy-start.1 = (f32[8,54,4,1]{3,0,1,2:T(8,128)S(1)}, f32[8,54,4,1]{3,0,1,2:T(8,128)}, u32[]{:S(2)}) copy-start(f32[8,54,4,1]{3,0,1,2:T(8,128)} %get-tuple-element.102) | copy-start | bytes 20740
  174.4 15.0 %collective-permute-start.13 = (f32[8,54,4,1]{1,0,3,2:T(8,128)}, f32[8,54,4,1]{1,0,3,2:T(8,128)}, u32[]{:S(2)}, u32[]{:S(2)}) collective-permute-start(f32[8,54,4,1]{1,0,3,2:T(8,128)} %copy.237), channel_id=1, source_target_pairs={{0,1},{2,3},{4,5},{6,7},{8,9},{10,11},{12,13},{14,15},{16,17},{18,... | collective-permute-start | bytes 20744 | tf_op jit(solution)/shard_map/ppermute | solution.py:27
  177.3 13.2 %collective-permute-start.12 = (f32[8,54,4,1]{1,0,3,2:T(8,128)}, f32[8,54,4,1]{1,0,3,2:T(8,128)S(1)}, u32[]{:S(2)}, u32[]{:S(2)}) collective-permute-start(f32[8,54,4,1]{1,0,3,2:T(8,128)} %copy.235), channel_id=1, source_target_pairs={{1,0},{3,2},{5,4},{7,6},{9,8},{11,10},{13,12},{15,14},{17,16},{19,... | collective-permute-start | bytes 20744 | tf_op jit(solution)/shard_map/ppermute | solution.py:28
  178.6 13.4 %collective-permute-start.11 = (f32[8,54,1,128]{3,0,1,2:T(8,128)}, f32[8,54,1,128]{3,0,1,2:T(8,128)S(1)}, u32[]{:S(2)}, u32[]{:S(2)}) collective-permute-start(f32[8,54,1,128]{3,0,1,2:T(8,128)} %get-tuple-element.101), channel_id=1, source_target_pairs={{0,2},{2,4},{4,6},{6,8},{8,10},{10,12},{12,14},{14,0},{1,3},{3,5},... | collective-permute-start | bytes 663560 | tf_op jit(solution)/shard_map/ppermute | solution.py:27
  181.3 13.2 %collective-permute-start.10 = (f32[8,54,1,128]{3,0,1,2:T(8,128)}, f32[8,54,1,128]{3,0,1,2:T(8,128)}, u32[]{:S(2)}, u32[]{:S(2)}) collective-permute-start(f32[8,54,1,128]{3,0,1,2:T(8,128)} %get-tuple-element.100), channel_id=1, source_target_pairs={{2,0},{4,2},{6,4},{8,6},{10,8},{12,10},{14,12},{0,14},{3,1},{5,3},... | collective-permute-start | bytes 663560 | tf_op jit(solution)/shard_map/ppermute | solution.py:28
  187.1 9.8 %collective-permute-start.14 = (f32[8,2,4,128]{3,0,1,2:T(8,128)}, f32[8,2,4,128]{3,0,1,2:T(8,128)}, u32[]{:S(2)}, u32[]{:S(2)}) collective-permute-start(f32[8,2,4,128]{3,0,1,2:T(8,128)} %pad_maximum_fusion.14), channel_id=1, source_target_pairs={{0,16},{16,0},{1,17},{17,1},{2,18},{18,2},{3,19},{19,3},{4,20},{20... | collective-permute-start | bytes 98312 | tf_op jit(solution)/shard_map/ppermute | solution.py:17
  192.0 0.7 copy-start.10
  242.4 1.2 copy-start.5
  243.6 1.8 copy-start.3
  244.5 1.0 copy-start.4
  245.4 1.1 slice-start.2
  246.6 1.2 slice-start
  247.8 1.4 slice-start.3
  249.2 0.9 slice-start.1
where the time goes:
time: 252 us; the launch traced here: 251 us
  blocking collectives  115 us (46%)
  local copies, waits for them, and re-layouts  36.6 us (15%)
  matrix products  36.5 us (14%)
  starting transfers between devices  31.1 us (12%)
  other arithmetic  28.4 us (11%)
    psum x2, blocking collectives, per_device(): lax.psum((moments_local(direction_core, image_set), moments_local(image_s...  76.4 us
    psum x1, blocking collectives, per_device(): lax.psum(moments_local(start_core, start_core), ('grp', 'az', 'ax'))  38.6 us
    dot_general x14, matrix products, products(): jnp.einsum('vrax,wrax->vw', first_set, second_set, precision=exact_mode)  15.5 us
    ppermute x6, starting transfers between devices, extended(): before = lax.ppermute(last, axis, up)  13.6 us
    unnamed x50, local copies, waits for them, and re-layouts  12 us
    ppermute x6, starting transfers between devices, extended(): after = lax.ppermute(first, axis, down)  11.4 us
    dot_general x8, matrix products, combine(): return jnp.einsum('vrax,vw->wrax', vector_set, mixing, precision=exact_mode)  9.04 us
    dot_general x3, matrix products, column_part(): jnp.einsum('rs,vsc->vrc', matrix, flat_set, precision=exact_mode)  8.66 us
  transfers between devices with their start and end apart: 15, of which 2 were waited for; matrix products, arithmetic and copies ran while one was open for 14% of the time, Pallas kernels for 0%

commit v1 on v0

--- a/solution.py
+++ b/solution.py
@@ -105,7 +105,8 @@
     direction = right_side
     solution = jnp.zeros_like(right_side)
     start_core = residual
-    norms_now = lax.psum(moments_local(start_core, start_core), ("grp", "az", "ax"))
+    one_axis = lax.psum(moments_local(start_core, start_core), ("az", "ax"))
+    norms_now = lax.psum(one_axis, "grp")
     for sweep in range(ITERS):
         image_set = apply_shallow(direction, matrix, diagonal_own, wet_area, layout)
         direction_core = direction

time: 252 us -> 289 us (1.15)
  blocking collectives: 115 us -> 151 us
    psum x2 -> x3, blocking collectives: 76.4 us -> 114 us  [per_device(): lax.psum((moments_local(direction_core, image_set), moments_local(image_s...]
    psum x1 -> x2, blocking collectives: 38.6 us -> 36.2 us  [the longest x1 31.3 us: per_device(): one_axis = lax.psum(moments_local(start_core, start_core), ('az', 'ax'))]
    unnamed x50 -> x54, local copies, waits for them, and re-layouts: 12 us -> 12.8 us
  transfers between devices with their start and end apart: 15 -> 15, of which waited for: 2 -> 2; matrix products, arithmetic and copies ran while one was open for 14% -> 13% of each run, Pallas kernels for 0% -> 0%
where the time goes in v1:
time: 289 us; the launch traced here: 287 us
  blocking collectives  151 us (52%)
  local copies, waits for them, and re-layouts  37.6 us (13%)
  matrix products  35.8 us (12%)
  starting transfers between devices  31.2 us (11%)
  other arithmetic  28.9 us (10%)
    psum x3, blocking collectives, per_device(): lax.psum((moments_local(direction_core, image_set), moments_local(image_s...  114 us
    psum x1, blocking collectives, per_device(): one_axis = lax.psum(moments_local(start_core, start_core), ('az', 'ax'))  31.3 us
    dot_general x14, matrix products, products(): jnp.einsum('vrax,wrax->vw', first_set, second_set, precision=exact_mode)  14.9 us
    ppermute x6, starting transfers between devices, extended(): before = lax.ppermute(last, axis, up)  13.6 us
    unnamed x54, local copies, waits for them, and re-layouts  12.8 us
    ppermute x6, starting transfers between devices, extended(): after = lax.ppermute(first, axis, down)  11.5 us
    dot_general x8, matrix products, combine(): return jnp.einsum('vrax,vw->wrax', vector_set, mixing, precision=exact_mode)  9.06 us
    dot_general x3, matrix products, column_part(): jnp.einsum('rs,vsc->vrc', matrix, flat_set, precision=exact_mode)  8.66 us
  transfers between devices with their start and end apart: 15, of which 2 were waited for; matrix products, arithmetic and copies ran while one was open for 13% of the time, Pallas kernels for 0%

profile of v1, /device:TPU:0, one launch (start us, length us, event | category | flops | bytes accessed | tf_op | source)
XLA Modules:
  0.0 287.2 jit_solution(8119723324928239516)
XLA Ops:
  0.6 2.5 fusion.124
  4.1 1.0 copy.166
  5.1 2.4 collective-permute-start.3
  7.9 1.3 collective-permute-start.2
  9.2 2.4 collective-permute-start.1
  11.6 3.1 %collective-permute-start = (f32[8,54,1,128]{3,0,1,2:T(8,128)S(1)}, f32[8,54,1,128]{3,0,1,2:T(8,128)}, u32[]{:S(2)}, u32[]{:S(2)}) collective-permute-start(f32[8,54,1,128]{3,0,1,2:T(8,128)S(1)} %get-tuple-element.109), channel_id=1, source_target_pairs={{2,0},{4,2},{6,4},{8,6},{10,8},{12,10},{14,12},{0,14},{3,1},{5,3},... | collective-permute-start | bytes 663560 | tf_op jit(solution)/shard_map/ppermute | solution.py:28
  16.1 1.6 collective-permute-start.4
  17.7 1.9 convolution_bitcast_fusion.3
  20.0 31.3 %psum.64 = f32[8,8]{0,1:T(8,128)S(1)} all-reduce(f32[8,8]{0,1:T(8,128)S(1)} %fusion.13), channel_id=1, replica_groups=mesh['grp'=2,'az'=8,'ax'=2] {'az','ax'}, use_global_device_ids=true, to_apply=%region_3.0 | all-reduce | flops 64 | bytes 512 | tf_op jit(solution)/shard_map/psum | solution.py:108
  51.2 4.9 %psum.65 = f32[8,8]{0,1:T(8,128)S(1)} all-reduce(f32[8,8]{0,1:T(8,128)S(1)} %psum.64), channel_id=1, replica_groups=mesh['grp'=2,'az'=8,'ax'=2] {'grp'}, use_global_device_ids=true, to_apply=%region_4.0 | all-reduce | flops 64 | bytes 512 | tf_op jit(solution)/shard_map/psum | solution.py:109
  58.5 2.4 convolution_bitcast_fusion.2
  61.6 1.2 custom-call.19
  62.8 1.4 copy.167
  64.2 1.4 copy.165
  66.3 2.3 fusion.26
  70.8 1.9 convolution_bitcast_fusion.15
  72.7 1.8 convolution_bitcast_fusion.13
  75.1 37.2 %all-reduce.3 = (f32[8,8]{1,0:T(8,128)S(1)}, f32[8,8]{0,1:T(8,128)S(1)}, f32[8,8]{0,1:T(8,128)S(1)}) all-reduce(f32[8,8]{1,0:T(8,128)S(1)} %bitcast.241, f32[8,8]{0,1:T(8,128)S(1)} %fusion.11, f32[8,8]{0,1:T(8,128)S(1)} %fusion.9), channel_id=1, replica_groups=mesh['grp'=2,'az'=8,'ax'=2] {'grp','az','ax'}, use_global_device_ids=true, to_apply=%region_0.1 | all-reduce | flops 192 | bytes 1536 | tf_op jit(solution)/shard_map/psum | solution.py:114
  115.5 1.9 fusion.31
  117.4 0.9 convolution_subtract_fusion.2
  119.9 0.9 convolution_add_fusion.3
  120.8 1.2 fusion.121
  122.0 0.8 fusion.120
  124.2 2.1 copy.206
  126.3 1.9 collective-permute-start.8
  128.2 1.0 copy.204
  129.2 1.3 collective-permute-start.7
  130.5 2.3 collective-permute-start.6
  132.8 2.4 collective-permute-start.5
  135.2 3.1 %convolution_bitcast_fusion.1 = f32[8,54,512]{2,1,0:T(8,128)} fusion(f32[8,54,512]{2,0,1:T(8,128)S(1)} %bitcast.235, f32[6,6]{1,0:T(8,128)S(1)} %copy-done.16, f32[48,48]{1,0:T(8,128)} %bitcast.238), kind=kOutput, calls=%fused_computation.1 | convolution fusion | flops 143341808 | bytes 1778832 | tf_op jit(solution)/shard_map/rs,vsc->vrc/dot_general | solution.py:49
  139.0 2.3 collective-permute-start.9
  143.3 1.2 custom-call.23
  144.5 1.1 copy.207
  145.7 1.4 copy.205
  147.7 2.5 fusion.22
  151.7 1.8 convolution_bitcast_fusion.11
  153.5 1.8 convolution_bitcast_fusion.9
  155.3 1.8 convolution_bitcast_fusion.7
  158.0 39.1 %all-reduce.2 = (f32[8,8]{0,1:T(8,128)S(1)}, f32[8,8]{0,1:T(8,128)}, f32[8,8]{0,1:T(8,128)}) all-reduce(f32[8,8]{0,1:T(8,128)S(1)} %fusion.7, f32[8,8]{0,1:T(8,128)S(1)} %fusion.5, f32[8,8]{0,1:T(8,128)S(1)} %fusion.3), channel_id=1, replica_groups=mesh['grp'=2,'az'=8,'ax'=2] {'grp','az','ax'}, use_global_device_ids=true, to_apply=%region_7.11 | all-reduce | flops 192 | bytes 1536 | tf_op jit(solution)/shard_map/psum | solution.py:114
  200.2 0.9 convolution_subtract_fusion.1
  203.1 0.9 convolution_add_fusion.1
  204.0 1.5 fusion.119
  206.4 1.1 copy-done.3
  207.5 1.9 convolution_add_fusion.2
  209.3 2.2 copy.237
  211.6 2.0 collective-permute-start.13
  213.5 1.0 copy.235
  214.5 1.3 collective-permute-start.12
  215.8 2.7 collective-permute-start.11
  218.5 2.1 collective-permute-start.10
  220.6 3.1 %convolution_bitcast_fusion = f32[8,54,512]{2,1,0:T(8,128)} fusion(f32[8,54,512]{2,0,1:T(8,128)S(1)} %bitcast.236, f32[6,6]{1,0:T(8,128)S(1)} %copy-done.16, f32[48,48]{1,0:T(8,128)} %bitcast.239), kind=kOutput, calls=%fused_computation | convolution fusion | flops 143341808 | bytes 1778832 | tf_op jit(solution)/shard_map/rs,vsc->vrc/dot_general | solution.py:49
  224.3 2.2 collective-permute-start.14
  226.5 1.1 copy.238
  227.7 1.4 copy.236
  229.9 1.8 collective-permute-done.10
  231.7 2.4 fusion.18
  235.7 1.8 convolution_bitcast_fusion.5
  237.7 38.0 %psum.71 = f32[8,8]{0,1:T(8,128)S(1)} all-reduce(f32[8,8]{0,1:T(8,128)S(1)} %fusion.1), channel_id=1, replica_groups=mesh['grp'=2,'az'=8,'ax'=2] {'grp','az','ax'}, use_global_device_ids=true, to_apply=%region_10.14 | all-reduce | flops 64 | bytes 512 | tf_op jit(solution)/shard_map/psum | solution.py:114
  278.9 0.9 convolution_subtract_fusion
  280.1 0.8 convolution_add_fusion
  280.9 1.0 copy-done.5
  281.9 1.1 slice-done.2
  283.0 1.1 copy.249
  284.2 1.4 copy.250
  (155 shorter events, 35.8 us)
Async XLA Ops:
  0.6 2.5 copy-start.7
  5.1 57.7 %collective-permute-start.3 = (f32[8,54,4,1]{1,0,3,2:T(8,128)}, f32[8,54,4,1]{1,0,3,2:T(8,128)S(1)}, u32[]{:S(2)}, u32[]{:S(2)}) collective-permute-start(f32[8,54,4,1]{1,0,3,2:T(8,128)} %copy.166), channel_id=1, source_target_pairs={{0,1},{2,3},{4,5},{6,7},{8,9},{10,11},{12,13},{14,15},{16,17},{18,... | collective-permute-start | bytes 20744 | tf_op jit(solution)/shard_map/ppermute | solution.py:27
  7.5 10.2 %copy-start = (f32[8,48,4,128]{3,2,1,0:T(4,128)S(1)}, f32[8,48,4,128]{3,2,1,0:T(4,128)}, u32[]{:S(2)}) copy-start(f32[8,48,4,128]{3,2,1,0:T(4,128)} %param.24) | copy-start | bytes 2359300
  7.9 56.3 %collective-permute-start.2 = (f32[8,54,4,1]{1,0,3,2:T(8,128)S(1)}, f32[8,54,4,1]{1,0,3,2:T(8,128)S(1)}, u32[]{:S(2)}, u32[]{:S(2)}) collective-permute-start(f32[8,54,4,1]{1,0,3,2:T(8,128)S(1)} %copy.164), channel_id=1, source_target_pairs={{1,0},{3,2},{5,4},{7,6},{9,8},{11,10},{13,12},{15,14},{17,16},{19,... | collective-permute-start | bytes 20744 | tf_op jit(solution)/shard_map/ppermute | solution.py:28
  9.2 56.4 %collective-permute-start.1 = (f32[8,54,1,128]{3,0,1,2:T(8,128)S(1)}, f32[8,54,1,128]{3,0,1,2:T(8,128)S(1)}, u32[]{:S(2)}, u32[]{:S(2)}) collective-permute-start(f32[8,54,1,128]{3,0,1,2:T(8,128)S(1)} %get-tuple-element.110), channel_id=1, source_target_pairs={{0,2},{2,4},{4,6},{6,8},{8,10},{10,12},{12,14},{14,0},{1,3},{3,5},... | collective-permute-start | bytes 663560 | tf_op jit(solution)/shard_map/ppermute | solution.py:27
  11.6 54.7 %collective-permute-start = (f32[8,54,1,128]{3,0,1,2:T(8,128)S(1)}, f32[8,54,1,128]{3,0,1,2:T(8,128)}, u32[]{:S(2)}, u32[]{:S(2)}) collective-permute-start(f32[8,54,1,128]{3,0,1,2:T(8,128)S(1)} %get-tuple-element.109), channel_id=1, source_target_pairs={{2,0},{4,2},{6,4},{8,6},{10,8},{12,10},{14,12},{0,14},{3,1},{5,3},... | collective-permute-start | bytes 663560 | tf_op jit(solution)/shard_map/ppermute | solution.py:28
  16.1 52.5 %collective-permute-start.4 = (f32[8,2,4,128]{3,0,1,2:T(8,128)}, f32[8,2,4,128]{3,0,1,2:T(8,128)}, u32[]{:S(2)}, u32[]{:S(2)}) collective-permute-start(f32[8,2,4,128]{3,0,1,2:T(8,128)} %pad_maximum_fusion.12), channel_id=1, source_target_pairs={{0,16},{16,0},{1,17},{17,1},{2,18},{18,2},{3,19},{19,3},{4,20},{20... | collective-permute-start | bytes 98312 | tf_op jit(solution)/shard_map/ppermute | solution.py:17
  51.2 7.2 %copy-start.9 = (f32[1,48,48]{2,1,0:T(8,128)S(1)}, f32[1,48,48]{2,1,0:T(8,128)}, u32[]{:S(2)}) copy-start(f32[1,48,48]{2,1,0:T(8,128)} %param.26) | copy-start | bytes 27652
  57.7 0.7 copy-start.16
  58.5 2.4 copy-start.23
  58.5 2.4 copy-start.13
  58.5 2.4 copy-start.21
  61.6 4.7 %copy-start.1 = (f32[8,54,512]{2,1,0:T(8,128)S(1)}, f32[8,54,512]{2,1,0:T(8,128)}, u32[]{:S(2)}) copy-start(f32[8,54,512]{2,1,0:T(8,128)} %convolution_bitcast_fusion.2) | copy-start | bytes 2654212
  65.6 0.7 copy-start.10
  72.7 1.8 copy-start.8
  118.8 0.7 copy-start.17
  126.3 18.3 %collective-permute-start.8 = (f32[8,54,4,1]{1,0,3,2:T(8,128)}, f32[8,54,4,1]{1,0,3,2:T(8,128)}, u32[]{:S(2)}, u32[]{:S(2)}) collective-permute-start(f32[8,54,4,1]{1,0,3,2:T(8,128)} %copy.206), channel_id=1, source_target_pairs={{0,1},{2,3},{4,5},{6,7},{8,9},{10,11},{12,13},{14,15},{16,17},{18,... | collective-permute-start | bytes 20744 | tf_op jit(solution)/shard_map/ppermute | solution.py:27
  129.2 16.5 %collective-permute-start.7 = (f32[8,54,4,1]{1,0,3,2:T(8,128)}, f32[8,54,4,1]{1,0,3,2:T(8,128)S(1)}, u32[]{:S(2)}, u32[]{:S(2)}) collective-permute-start(f32[8,54,4,1]{1,0,3,2:T(8,128)} %copy.204), channel_id=1, source_target_pairs={{1,0},{3,2},{5,4},{7,6},{9,8},{11,10},{13,12},{15,14},{17,16},{19,... | collective-permute-start | bytes 20744 | tf_op jit(solution)/shard_map/ppermute | solution.py:28
  130.5 16.6 %collective-permute-start.6 = (f32[8,54,1,128]{3,0,1,2:T(8,128)}, f32[8,54,1,128]{3,0,1,2:T(8,128)S(1)}, u32[]{:S(2)}, u32[]{:S(2)}) collective-permute-start(f32[8,54,1,128]{3,0,1,2:T(8,128)} %get-tuple-element.106), channel_id=1, source_target_pairs={{0,2},{2,4},{4,6},{6,8},{8,10},{10,12},{12,14},{14,0},{1,3},{3,5},... | collective-permute-start | bytes 663560 | tf_op jit(solution)/shard_map/ppermute | solution.py:27
  132.8 14.9 %collective-permute-start.5 = (f32[8,54,1,128]{3,0,1,2:T(8,128)}, f32[8,54,1,128]{3,0,1,2:T(8,128)}, u32[]{:S(2)}, u32[]{:S(2)}) collective-permute-start(f32[8,54,1,128]{3,0,1,2:T(8,128)} %get-tuple-element.105), channel_id=1, source_target_pairs={{2,0},{4,2},{6,4},{8,6},{10,8},{12,10},{14,12},{0,14},{3,1},{5,3},... | collective-permute-start | bytes 663560 | tf_op jit(solution)/shard_map/ppermute | solution.py:28
  135.2 3.1 %copy-start.14 = (f32[8,1,4,128]{3,0,1,2:T(8,128)S(1)}, f32[8,1,4,128]{3,0,1,2:T(8,128)}, u32[]{:S(2)}) copy-start(f32[8,1,4,128]{3,0,1,2:T(8,128)} %get-tuple-element.103) | copy-start | bytes 49156
  135.2 3.1 %copy-start.15 = (f32[8,1,4,128]{3,0,1,2:T(8,128)S(1)}, f32[8,1,4,128]{3,0,1,2:T(8,128)}, u32[]{:S(2)}) copy-start(f32[8,1,4,128]{3,0,1,2:T(8,128)} %get-tuple-element.104) | copy-start | bytes 49156
  138.4 2.9 %copy-start.19 = (f32[8,8]{1,0:T(8,128)S(1)}, f32[8,8]{1,0:T(8,128)}, u32[]{:S(2)}) copy-start(f32[8,8]{1,0:T(8,128)} %copy.218) | copy-start | bytes 772
  139.0 11.2 %collective-permute-start.9 = (f32[8,2,4,128]{3,0,1,2:T(8,128)}, f32[8,2,4,128]{3,0,1,2:T(8,128)}, u32[]{:S(2)}, u32[]{:S(2)}) collective-permute-start(f32[8,2,4,128]{3,0,1,2:T(8,128)} %pad_maximum_fusion.13), channel_id=1, source_target_pairs={{0,16},{16,0},{1,17},{17,1},{2,18},{18,2},{3,19},{19,3},{4,20},{20... | collective-permute-start | bytes 98312 | tf_op jit(solution)/shard_map/ppermute | solution.py:17
  147.1 0.7 copy-start.11
  200.2 0.9 copy-start.20
  201.2 0.7 copy-start.22
  202.0 0.7 copy-start.18
  206.3 1.2 copy-start.3
  209.3 4.2 %copy-start.2 = (f32[8,54,4,1]{3,0,1,2:T(8,128)S(1)}, f32[8,54,4,1]{3,0,1,2:T(8,128)}, u32[]{:S(2)}) copy-start(f32[8,54,4,1]{3,0,1,2:T(8,128)} %get-tuple-element.101) | copy-start | bytes 20740
  211.6 15.0 %collective-permute-start.13 = (f32[8,54,4,1]{1,0,3,2:T(8,128)}, f32[8,54,4,1]{1,0,3,2:T(8,128)}, u32[]{:S(2)}, u32[]{:S(2)}) collective-permute-start(f32[8,54,4,1]{1,0,3,2:T(8,128)} %copy.237), channel_id=1, source_target_pairs={{0,1},{2,3},{4,5},{6,7},{8,9},{10,11},{12,13},{14,15},{16,17},{18,... | collective-permute-start | bytes 20744 | tf_op jit(solution)/shard_map/ppermute | solution.py:27
  214.5 13.2 %collective-permute-start.12 = (f32[8,54,4,1]{1,0,3,2:T(8,128)}, f32[8,54,4,1]{1,0,3,2:T(8,128)S(1)}, u32[]{:S(2)}, u32[]{:S(2)}) collective-permute-start(f32[8,54,4,1]{1,0,3,2:T(8,128)} %copy.235), channel_id=1, source_target_pairs={{1,0},{3,2},{5,4},{7,6},{9,8},{11,10},{13,12},{15,14},{17,16},{19,... | collective-permute-start | bytes 20744 | tf_op jit(solution)/shard_map/ppermute | solution.py:28
  215.8 13.4 %collective-permute-start.11 = (f32[8,54,1,128]{3,0,1,2:T(8,128)}, f32[8,54,1,128]{3,0,1,2:T(8,128)S(1)}, u32[]{:S(2)}, u32[]{:S(2)}) collective-permute-start(f32[8,54,1,128]{3,0,1,2:T(8,128)} %get-tuple-element.100), channel_id=1, source_target_pairs={{0,2},{2,4},{4,6},{6,8},{8,10},{10,12},{12,14},{14,0},{1,3},{3,5},... | collective-permute-start | bytes 663560 | tf_op jit(solution)/shard_map/ppermute | solution.py:27
  218.5 13.2 %collective-permute-start.10 = (f32[8,54,1,128]{3,0,1,2:T(8,128)}, f32[8,54,1,128]{3,0,1,2:T(8,128)}, u32[]{:S(2)}, u32[]{:S(2)}) collective-permute-start(f32[8,54,1,128]{3,0,1,2:T(8,128)} %get-tuple-element.99), channel_id=1, source_target_pairs={{2,0},{4,2},{6,4},{8,6},{10,8},{12,10},{14,12},{0,14},{3,1},{5,3},... | collective-permute-start | bytes 663560 | tf_op jit(solution)/shard_map/ppermute | solution.py:28
  224.3 9.9 %collective-permute-start.14 = (f32[8,2,4,128]{3,0,1,2:T(8,128)}, f32[8,2,4,128]{3,0,1,2:T(8,128)}, u32[]{:S(2)}, u32[]{:S(2)}) collective-permute-start(f32[8,2,4,128]{3,0,1,2:T(8,128)} %pad_maximum_fusion.14), channel_id=1, source_target_pairs={{0,16},{16,0},{1,17},{17,1},{2,18},{18,2},{3,19},{19,3},{4,20},{20... | collective-permute-start | bytes 98312 | tf_op jit(solution)/shard_map/ppermute | solution.py:17
  229.2 0.7 copy-start.12
  278.9 1.2 copy-start.6
  280.1 1.8 copy-start.4
  280.9 1.0 copy-start.5
  281.9 1.1 slice-start.2
  283.0 1.2 slice-start
  284.2 1.4 slice-start.3
  285.6 0.9 slice-start.1
